TPU v7x, 32 devices: a whole 2x2x4 slice. The times are simulated.
32 devices in a mesh: fields: 2 (over x), rows: 16 (over z, y, core).
Axes of the slice: x: 2, y: 2, z: 4, core: 2. Of those that a mesh axis runs over, the one named last changes fastest.
Arguments:
- members: bfloat16 [512, 131072], P('rows', 'fields'), parts along dimension 1, may hold values from -6 to 6
- predicted: bfloat16 [512, 32768], P('rows', 'fields'), parts along dimension 1, may hold values from -6 to 6
- noise: bfloat16 [512, 32768], P('rows', 'fields'), parts along dimension 1, may hold values from -6 to 6
- observed: float32 [32768], P(('fields', 'rows')), parts along dimension 0, may hold values from -12 to 12
- observation_spread: float32 [32768], P(('fields', 'rows')), parts along dimension 0, may hold values from 1 to 16
Outputs:
- updated: bfloat16 [512, 131072], P('rows', 'fields'), parts along dimension 1
There are 2 independent parts, one for each index of `fields`. A program takes and returns all parts, laid end to end along the dimension named above; each array names one. Nothing has to cross between parts.
All inputs are finite; a program needn't handle non-finite values.
Results may differ from a plain program's by a relative error of at most 0.005.
Values may be sent and summed in bfloat16 or wider, within the bound.
A program may use at most 64 MiB of HBM per device.

v0:
```python
import math

import jax
import jax.numpy as jnp
from jax import lax
from jax.sharding import PartitionSpec as P

NE = 512


damping = 21.0


def on_device(members, predicted, noise, observed, observation_spread):
    row_count = lax.axis_size("rows")
    local_count = members.shape[0]
    cells_here = members.shape[1] // row_count
    inverse_square_root = 1.0 / math.sqrt(NE - 1)
    predicted_response, random_jitter = (
        lax.all_to_all(predicted, "rows", split_axis=1, concat_axis=0, tiled=True),
        lax.all_to_all(noise, "rows", split_axis=1, concat_axis=0, tiled=True),
    )
    predicted_response = predicted_response.astype(jnp.float32)
    ensemble_data_average = jnp.mean(predicted_response, axis=0)
    standardized_anomalies = (
        (predicted_response - ensemble_data_average) * (inverse_square_root / observation_spread)
    ).astype(jnp.bfloat16)
    measurement_residual = (
        (observed - predicted_response) / observation_spread + random_jitter.astype(jnp.float32)
    ).astype(jnp.bfloat16)
    gram_matrix = lax.dot_general(
        standardized_anomalies,
        standardized_anomalies,
        (((1,), (1,)), ((), ())),
        preferred_element_type=jnp.float32,
    )
    cross_terms = lax.dot_general(
        standardized_anomalies,
        measurement_residual,
        (((1,), (1,)), ((), ())),
        preferred_element_type=jnp.float32,
    )
    identity = jnp.eye(NE, dtype=jnp.float32)
    gram_total, cross_total = lax.psum((gram_matrix, cross_terms), "rows")
    factor = jnp.linalg.cholesky(gram_total + damping * identity)
    weights = jax.scipy.linalg.cho_solve((factor, True), cross_total).astype(jnp.bfloat16)
    blocks = members.reshape(local_count, row_count, cells_here)
    params = lax.all_to_all(blocks, "rows", split_axis=1, concat_axis=0, tiled=True)[
        :, 0, :
    ].astype(jnp.float32)
    cell_mean = jnp.mean(params, axis=0)
    anomaly = ((params - cell_mean) * inverse_square_root).astype(jnp.bfloat16)
    update = lax.dot_general(
        weights, anomaly, (((0,), (0,)), ((), ())), preferred_element_type=jnp.float32
    )
    renewed = (params + update).astype(jnp.bfloat16)[:, None, :]
    result = lax.all_to_all(renewed, "rows", split_axis=0, concat_axis=1, tiled=True)
    return result.reshape(local_count, row_count * cells_here)


def solution(mesh):
    in_specs = (
        P("rows", "fields"),
        P("rows", "fields"),
        P("rows", "fields"),
        P(("fields", "rows")),
        P(("fields", "rows")),
    )
    out_specs = P("rows", "fields")
    return jax.shard_map(
        on_device, mesh=mesh, in_specs=in_specs, out_specs=out_specs, check_vma=False
    )
```

profile of v0, /device:TPU:13, one launch (start us, length us, event | category | flops | bytes accessed | tf_op | source)
XLA Modules:
  0.0 533.8 jit_solution(1791297434212746293)
XLA Ops:
  6.5 2.4 copy.103
  8.9 6.7 %all-to-all-start.1 = ((bf16[32,16,1024]{2,0,1:T(8,128)(2,1)}), bf16[32,16,1024]{2,0,1:T(8,128)(2,1)S(1)}, u32[]{:S(2)}, u32[]{:S(2)}) async-start(bf16[32,16,1024]{2,0,1:T(8,128)(2,1)} %bitcast.103), calls=%async_computation.1 | async-start | bytes 2097152 | tf_op jit(solution)/shard_map/all_to_all | solution.py:20
  16.7 23.8 %all-to-all-done.1 = bf16[32,16,1024]{2,0,1:T(8,128)(2,1)S(1)} async-done(((bf16[32,16,1024]{2,0,1:T(8,128)(2,1)}), bf16[32,16,1024]{2,0,1:T(8,128)(2,1)S(1)}, u32[]{:S(2)}, u32[]{:S(2)}) %all-to-all-start.1) | async-done | bytes 1048608 | tf_op jit(solution)/shard_map/all_to_all | solution.py:20
  40.4 4.8 all-to-all-start.2
  45.5 24.6 %all-to-all-done.2 = bf16[32,16,1024]{2,0,1:T(8,128)(2,1)S(1)} async-done(((bf16[32,16,1024]{2,0,1:T(8,128)(2,1)}), bf16[32,16,1024]{2,0,1:T(8,128)(2,1)S(1)}, u32[]{:S(2)}, u32[]{:S(2)}) %all-to-all-start.2) | async-done | bytes 1048608 | tf_op jit(solution)/shard_map/all_to_all | solution.py:21
  70.7 1.7 fusion.67
  72.5 1.7 fusion.68
  74.2 4.7 copy.101
  78.9 5.3 all-to-all-start
  84.3 143.1 %all-reduce.4.cloned.1.call-done = (f32[512,512]{1,0:T(8,128)}, f32[512,512]{0,1:T(8,128)}) async-done(((f32[512,512]{1,0:T(8,128)}, f32[512,512]{0,1:T(8,128)}), (f32[512,512]{1,0:T(8,128)}, f32[512,512]{0,1:T(8,128)})) %all-reduce.4.cloned.1.call-update) | async-done | bytes 2097168 | tf_op jit(solution)/shard_map/psum | solution.py:44
  227.4 1.4 select_add_fusion
  229.5 11.7 %cholesky.103 = f32[128,128]{1,0:T(8,128)S(1)} custom-call(f32[128,128]{1,0:T(8,128)S(1)} %cholesky.263), custom_call_target="Cholesky" | custom-call | tf_op jit(solution)/shard_map/jit(cholesky)/cholesky | solution.py:45
  241.2 9.8 %custom-call.34 = f32[1,128,128]{1,2,0:T(8,128)S(1)} custom-call(f32[1,128,128]{2,1,0:T(8,128)S(1)} %get-tuple-element.56), custom_call_target="InvertDiagBlocksLowerTriangular" | custom-call | tf_op jit(solution)/shard_map/jit(cholesky)/cholesky | solution.py:45
  251.9 11.7 %cholesky.215 = f32[128,128]{1,0:T(8,128)S(1)} custom-call(f32[128,128]{1,0:T(8,128)S(1)} %cholesky.267), custom_call_target="Cholesky" | custom-call | tf_op jit(solution)/shard_map/jit(cholesky)/cholesky | solution.py:45
  263.8 10.0 %custom-call.35 = f32[1,128,128]{1,2,0:T(8,128)S(1)} custom-call(f32[1,128,128]{2,1,0:T(8,128)S(1)} %get-tuple-element.54), custom_call_target="InvertDiagBlocksLowerTriangular" | custom-call | tf_op jit(solution)/shard_map/jit(cholesky)/cholesky | solution.py:45
  274.8 11.7 %cholesky.236 = f32[128,128]{1,0:T(8,128)S(1)} custom-call(f32[128,128]{1,0:T(8,128)S(1)} %cholesky.272), custom_call_target="Cholesky" | custom-call | tf_op jit(solution)/shard_map/jit(cholesky)/cholesky | solution.py:45
  286.7 9.8 %custom-call.36 = f32[1,128,128]{1,2,0:T(8,128)S(1)} custom-call(f32[1,128,128]{2,1,0:T(8,128)S(1)} %get-tuple-element.52), custom_call_target="InvertDiagBlocksLowerTriangular" | custom-call | tf_op jit(solution)/shard_map/jit(cholesky)/cholesky | solution.py:45
  297.3 11.9 %cholesky.253 = f32[128,128]{1,0:T(8,128)S(1)} custom-call(f32[128,128]{1,0:T(8,128)S(1)} %convolution_subtract_fusion.8), custom_call_target="Cholesky" | custom-call | tf_op jit(solution)/shard_map/jit(cholesky)/cholesky | solution.py:45
  314.1 8.6 %while.1 = (s32[]{:T(128)}, f32[512,512]{0,1:T(8,128)S(1)}, s32[4,2]{0,1:T(2,128)S(1)}, f32[4,128,128]{2,1,0:T(8,128)S(1)}, s32[]{:T(128)}) while((s32[]{:T(128)}, f32[512,512]{0,1:T(8,128)S(1)}, s32[4,2]{0,1:T(2,128)S(1)}, f32[4,128,128]{2,1,0:T(8,128)S(1)}, s32[]{:T(128)}) %tuple.33), condition=%wide.while_cond, body=%wide.while_body.sunk | while | flops 2 | bytes 393321 | solution.py:46
  322.7 39.3 %custom-call.37 = f32[4,128,128]{1,2,0:T(8,128)S(1)} custom-call(f32[4,128,128]{2,1,0:T(8,128)S(1)} %get-tuple-element.12), custom_call_target="InvertDiagBlocksLowerTriangular" | custom-call | tf_op jit(solution)/shard_map/jit(_cho_solve)/triangular_solve | solution.py:46
  362.0 1.4 fusion.33
  365.2 1.4 convolution_subtract_fusion.2
  367.1 1.6 convolution_subtract_fusion.5
  372.1 3.2 convert_reduce_fusion
  375.2 3.2 fusion.1
  378.5 6.7 %fusion.3 = bf16[512,1,4096]{2,0,1:T(8,128)(2,1)} fusion(bf16[512,4096]{1,0:T(8,128)(2,1)S(1)} %fusion.1, bf16[32,16,4096]{2,0,1:T(8,128)(2,1)} %all-to-all-done, bf16[128,512]{1,0:T(8,128)(2,1)S(1)} %get-tuple-element.57, bf16[128,512]{1,0:T(8,128)(2,1)S(1)} %get-tuple-element.59, bf16[128,512]{1,0:T(8,128)(2,1)S(1)} %get-tuple-element.61, ...), kind=kOutput, calls=%fused_computation.8 | convolution fusion | flops 2155872256 | bytes 13107200 | tf_op jit(solution)/shard_map/dot_general | solution.py:53
  385.6 6.7 %reduce.29 = bf16[512,4096]{1,0:T(8,128)(2,1)} reduce(bf16[512,1,4096]{2,0,1:T(8,128)(2,1)} %fusion.3, bf16[]{:T(256)} %broadcast.278), dimensions={1}, to_apply=%copy.86.reduce_sub_computation | reduce | bytes 8388610 | tf_op jit(solution)/shard_map/broadcast_in_dim | solution.py:56
  392.3 11.4 %reshape.144 = bf16[16,2,65536]{2,1,0:T(2,128)(2,1)} reshape(bf16[512,4096]{1,0:T(8,128)(2,1)} %reduce.29) | data formatting | bytes 8388608
  403.7 100.3 %all_to_all.50 = bf16[16,2,65536]{2,1,0:T(2,128)(2,1)} all-to-all(bf16[16,2,65536]{2,1,0:T(2,128)(2,1)} %reshape.144), channel_id=1, replica_groups=mesh['fields'=2,'rows'=16] {'rows'}, dimensions={0} | all-to-all | bytes 8388608 | tf_op jit(solution)/shard_map/all_to_all | solution.py:57
  504.0 12.3 %reshape.145 = bf16[512,1,4096]{2,1,0:T(2,128)(2,1)} reshape(bf16[16,2,65536]{2,1,0:T(2,128)(2,1)} %all_to_all.50) | data formatting | bytes 8388608
  516.3 8.1 %copy.92 = bf16[512,1,4096]{2,0,1:T(8,128)(2,1)S(1)} copy(bf16[512,1,4096]{2,1,0:T(2,128)(2,1)} %reshape.145) | data formatting | bytes 8388608
  524.4 2.3 copy.96
  (81 shorter events, 22.4 us)
Async XLA Ops:
  6.5 9.0 %copy-start.1 = (bf16[32,16384]{1,0:T(8,128)(2,1)S(1)}, bf16[32,16384]{1,0:T(8,128)(2,1)}, u32[]{:S(2)}) copy-start(bf16[32,16384]{1,0:T(8,128)(2,1)} %param.7) | copy-start | bytes 3145732
  6.5 38.8 %copy-start.2 = (f32[1024]{0:T(1024)S(1)}, f32[1024]{0:T(1024)}, u32[]{:S(2)}) copy-start(f32[1024]{0:T(1024)} %param.9) | copy-start | bytes 12292
  8.9 61.2 %copy-start.3 = (f32[1024]{0:T(1024)S(1)}, f32[1024]{0:T(1024)}, u32[]{:S(2)}) copy-start(f32[1024]{0:T(1024)} %param.8) | copy-start | bytes 12292
  8.9 31.5 %all-to-all-start.1 = ((bf16[32,16,1024]{2,0,1:T(8,128)(2,1)}), bf16[32,16,1024]{2,0,1:T(8,128)(2,1)S(1)}, u32[]{:S(2)}, u32[]{:S(2)}) async-start(bf16[32,16,1024]{2,0,1:T(8,128)(2,1)} %bitcast.103), calls=%async_computation.1 | async-start | bytes 2097152 | tf_op jit(solution)/shard_map/all_to_all | solution.py:20
  40.4 29.7 %all-to-all-start.2 = ((bf16[32,16,1024]{2,0,1:T(8,128)(2,1)}), bf16[32,16,1024]{2,0,1:T(8,128)(2,1)S(1)}, u32[]{:S(2)}, u32[]{:S(2)}) async-start(bf16[32,16,1024]{2,0,1:T(8,128)(2,1)} %bitcast.102), calls=%async_computation.2 | async-start | bytes 2097152 | tf_op jit(solution)/shard_map/all_to_all | solution.py:21
  45.3 182.2 %all-reduce.4.cloned.1.call-start = ((), (), s32[]{:S(2)}) async-start(), calls=%async_computation.4 | async-start | bytes 4194304 | tf_op jit(solution)/shard_map/psum | solution.py:44
  78.9 293.1 %all-to-all-start = ((bf16[32,16,4096]{2,0,1:T(8,128)(2,1)}), bf16[32,16,4096]{2,0,1:T(8,128)(2,1)}, u32[]{:S(2)}, u32[]{:S(2)}) async-start(bf16[32,16,4096]{2,0,1:T(8,128)(2,1)} %bitcast.111), calls=%async_computation | async-start | bytes 8388608 | tf_op jit(solution)/shard_map/all_to_all | solution.py:48
  227.4 1.8 copy-start
Sparse Core Ops, SparseCore 0:
  74.4 153.0 all-reduce.3
where the time goes:
time: 540 us; the launch traced here: 534 us
  waiting for transfers between devices  192 us (36%)
  other arithmetic  134 us (25%)
  blocking collectives  100 us (19%)
  local copies, waits for them, and re-layouts  52.2 us (10%)
  matrix products  22.4 us (4%)
  starting transfers between devices  16.8 us (3%)
  between operations  16.6 us (3%)
    psum x1, waiting for transfers between devices, on_device(): gram_total, cross_total = lax.psum((gram_matrix, cross_terms), 'rows')  143 us
    all_to_all x1, blocking collectives, on_device(): lax.all_to_all(renewed, 'rows', split_axis=0, concat_axis=1, tiled=True)  100 us
    another operation x14, other arithmetic, on_device(): factor = jnp.linalg.cholesky(gram_total + damping * identity)  78.8 us
    another operation x3, other arithmetic, on_device(): jax.scipy.linalg.cho_solve((factor, True), cross_total).astype(jnp.bfloat16)  39.5 us
    unnamed x12, local copies, waits for them, and re-layouts  34.1 us
    all_to_all x1, waiting for transfers between devices, on_device(): lax.all_to_all(noise, 'rows', split_axis=1, concat_axis=0, tiled=True)  24.6 us
    all_to_all x1, waiting for transfers between devices, on_device(): lax.all_to_all(predicted, 'rows', split_axis=1, concat_axis=0, tiled=True)  23.8 us
  transfers between devices with their start and end apart: 4, of which 3 were waited for; matrix products, arithmetic and copies ran while one was open for 28% of the time, Pallas kernels for 0%

commit v1 on v0

v1 whole, which is shorter than its diff:
```python
import functools
import math

import jax
import jax.numpy as jnp
from jax import lax
from jax.experimental import pallas as pl
from jax.experimental.pallas import tpu as pltpu
from jax.sharding import PartitionSpec as P

damping = 21.0
BLOCK = 128
HIGHEST = lax.Precision.HIGHEST


def sweep_block(m):
    size = m.shape[0]
    rows = lax.broadcasted_iota(jnp.int32, m.shape, 0)
    columns = lax.broadcasted_iota(jnp.int32, m.shape, 1)
    for k in range(size):
        row = m[k : k + 1, :]
        column = m[:, k : k + 1]
        inverse = 1.0 / m[k : k + 1, k : k + 1]
        scaled = row * inverse
        swept = m - column * scaled
        swept = jnp.where(columns == k, column * inverse, swept)
        edge = jnp.where(columns[k : k + 1] == k, -inverse, scaled)
        m = jnp.where(rows == k, edge, swept)
    return m


def solve_kernel(gram_ref, cross_t_ref, weights_t_ref, a_ref):
    ne = gram_ref.shape[0]
    eye = lax.broadcasted_iota(jnp.int32, (ne, ne), 0) == lax.broadcasted_iota(
        jnp.int32, (ne, ne), 1
    )
    a_ref[...] = gram_ref[...] + jnp.where(eye, damping, 0.0)

    def step(block, carry):
        here = pl.ds(pl.multiple_of(block * BLOCK, BLOCK), BLOCK)
        negative = sweep_block(a_ref[here, here])
        panel = a_ref[here, :]
        column = a_ref[:, here]
        scaled = -jnp.dot(negative, panel, precision=HIGHEST, preferred_element_type=jnp.float32)
        scaled_column = -jnp.dot(
            column, negative, precision=HIGHEST, preferred_element_type=jnp.float32
        )
        a_ref[...] = a_ref[...] - jnp.dot(
            column, scaled, precision=HIGHEST, preferred_element_type=jnp.float32
        )
        a_ref[here, :] = scaled
        a_ref[:, here] = scaled_column
        a_ref[here, here] = negative
        return carry

    lax.fori_loop(0, ne // BLOCK, step, 0)
    weights_t_ref[...] = (
        -jnp.dot(cross_t_ref[...], a_ref[...], precision=HIGHEST, preferred_element_type=jnp.float32)
    ).astype(jnp.bfloat16)


def solve(gram, cross_t):
    ne = gram.shape[0]
    return pl.pallas_call(
        solve_kernel,
        out_shape=jax.ShapeDtypeStruct((ne, ne), jnp.bfloat16),
        in_specs=[pl.BlockSpec(memory_space=pltpu.VMEM)] * 2,
        out_specs=pl.BlockSpec(memory_space=pltpu.VMEM),
        scratch_shapes=[pltpu.VMEM((ne, ne), jnp.float32)],
        compiler_params=pltpu.CompilerParams(vmem_limit_bytes=24 * 2**20),
        cost_estimate=pl.CostEstimate(
            flops=40 * ne**3, bytes_accessed=200 * 2**20, transcendentals=0
        ),
        name="solve",
    )(gram, cross_t)


def update_kernel(n, chunk, weights_t_ref, params_ref, out_ref, held, send_sem, recv_sem, own_sem):
    me = lax.axis_index("rows")
    ne, cells = params_ref.shape
    local = ne // n
    scale = 1.0 / math.sqrt(ne - 1)

    barrier = pltpu.get_barrier_semaphore()

    def greet(s, carry):
        pl.semaphore_signal(
            barrier,
            inc=1,
            device_id={"rows": lax.rem(me + s, n)},
            device_id_type=pl.DeviceIdType.MESH,
        )
        return carry

    lax.fori_loop(1, n, greet, 0)
    pl.semaphore_wait(barrier, n - 1)

    def outgoing(c, s):
        peer = lax.rem(me + s, n)
        return pltpu.make_async_remote_copy(
            src_ref=held.at[peer, :, pl.ds(pl.multiple_of(c * chunk, chunk), chunk)],
            dst_ref=out_ref.at[:, pl.ds(pl.multiple_of(me * cells + c * chunk, chunk), chunk)],
            send_sem=send_sem.at[c, s],
            recv_sem=recv_sem.at[c, s],
            device_id={"rows": peer},
            device_id_type=pl.DeviceIdType.MESH,
        )

    def own(c):
        return pltpu.make_async_copy(
            held.at[me, :, pl.ds(pl.multiple_of(c * chunk, chunk), chunk)],
            out_ref.at[:, pl.ds(pl.multiple_of(me * cells + c * chunk, chunk), chunk)],
            own_sem.at[c],
        )

    def compute(c, carry):
        here = pl.ds(pl.multiple_of(c * chunk, chunk), chunk)
        params = params_ref[:, here].astype(jnp.float32)
        mean = jnp.sum(params, axis=0, keepdims=True) * (1.0 / ne)
        anomaly = ((params - mean) * scale).astype(jnp.bfloat16)
        update = jnp.dot(weights_t_ref[...], anomaly, preferred_element_type=jnp.float32)
        held[:, :, here] = (params + update).reshape(n, local, chunk).astype(jnp.bfloat16)

        def send(s, carry):
            outgoing(c, s).start()
            return carry

        lax.fori_loop(1, n, send, 0)
        own(c).start()
        return carry

    count = cells // chunk
    lax.fori_loop(0, count, compute, 0)

    def finish(c, carry):
        def one(s, carry):
            outgoing(c, s).wait()
            return carry

        lax.fori_loop(1, n, one, 0)
        own(c).wait()
        return carry

    lax.fori_loop(0, count, finish, 0)


def update_and_send(weights_t, params, n):
    ne, cells = params.shape
    local = ne // n
    chunk = cells
    while chunk % 2 == 0 and chunk > 512:
        chunk //= 2
    count = cells // chunk
    return pl.pallas_call(
        functools.partial(update_kernel, n, chunk),
        out_shape=jax.ShapeDtypeStruct((local, n * cells), jnp.bfloat16),
        in_specs=[pl.BlockSpec(memory_space=pltpu.VMEM)] * 2,
        out_specs=pl.BlockSpec(memory_space=pl.ANY),
        scratch_shapes=[
            pltpu.VMEM((n, local, cells), jnp.bfloat16),
            pltpu.SemaphoreType.DMA((count, n)),
            pltpu.SemaphoreType.DMA((count, n)),
            pltpu.SemaphoreType.DMA((count,)),
        ],
        compiler_params=pltpu.CompilerParams(
            collective_id=0, has_side_effects=True, vmem_limit_bytes=40 * 2**20
        ),
        name="update",
    )(weights_t, params)


def on_device(members, predicted, noise, observed, observation_spread):
    n = lax.axis_size("rows")
    local = members.shape[0]
    ne = local * n
    cells = members.shape[1] // n
    scale = 1.0 / math.sqrt(ne - 1)
    predicted, noise = (
        lax.all_to_all(predicted, "rows", split_axis=1, concat_axis=0, tiled=True),
        lax.all_to_all(noise, "rows", split_axis=1, concat_axis=0, tiled=True),
    )
    params = lax.all_to_all(members, "rows", split_axis=1, concat_axis=0, tiled=True)
    predicted = predicted.astype(jnp.float32)
    mean = jnp.mean(predicted, axis=0)
    whitened = ((predicted - mean) * (scale / observation_spread)).astype(jnp.bfloat16)
    innovation = (
        (observed - predicted) / observation_spread + noise.astype(jnp.float32)
    ).astype(jnp.bfloat16)
    both = jnp.concatenate([whitened, innovation], axis=0)
    sums = lax.dot_general(
        both, whitened, (((1,), (1,)), ((), ())), preferred_element_type=jnp.float32
    )
    sums = lax.psum(sums, "rows")
    weights_t = solve(sums[:ne], sums[ne:])
    return update_and_send(weights_t, params, n)


def solution(mesh):
    in_specs = (
        P("rows", "fields"),
        P("rows", "fields"),
        P("rows", "fields"),
        P(("fields", "rows")),
        P(("fields", "rows")),
    )
    return jax.shard_map(
        on_device, mesh=mesh, in_specs=in_specs, out_specs=P("rows", "fields"), check_vma=False
    )
```

time: 540 us -> 402 us (0.74); the launches traced: 534 us -> 402 us
  Pallas kernels: 0 us -> 159 us
  other arithmetic: 134 us -> 0.81 us
  blocking collectives: 100 us -> 0 us
  local copies, waits for them, and re-layouts: 52.2 us -> 11.9 us
  matrix products: 22.4 us -> 2.64 us
  waiting for transfers between devices: 192 us -> 198 us
    pallas_call x0 -> x2, Pallas kernels: none -> 159 us  [the longest x1 101 us: update_and_send(): pl.pallas_call(functools.partial(update_kernel, n, chunk), out_shape=jax....]
    another operation x18 -> x0, other arithmetic: 119 us -> none  [the longest x14 78.8 us: on_device(): factor = jnp.linalg.cholesky(gram_total + damping * identity)]
    all_to_all x1 -> x0, blocking collectives: 100 us -> none  [on_device(): lax.all_to_all(renewed, 'rows', split_axis=0, concat_axis=1, tiled=True)]
    unnamed x12 -> x7, local copies, waits for them, and re-layouts: 34.1 us -> 2.03 us
    another operation x20 -> x0, matrix products: 12.2 us -> none  [the longest x14 9.91 us: on_device(): jax.scipy.linalg.cho_solve((factor, True), cross_total).astype(jnp.bfloat16)]
    psum x1, waiting for transfers between devices: 143 us -> 154 us  [on_device(): sums = lax.psum(sums, 'rows')]
    another operation x34 -> x0, local copies, waits for them, and re-layouts: 9.14 us -> none
    dot_general x3 -> x1, matrix products: 10.1 us -> 2.64 us  [on_device(): lax.dot_general(both, whitened, (((1,), (1,)), ((), ())), preferred_eleme...]
  transfers between devices with their start and end apart: 4 -> 4, of which waited for: 3 -> 3; matrix products, arithmetic and copies ran while one was open for 28% -> 3% of each run, Pallas kernels for 0% -> 14%
where the time goes in v1:
time: 402 us
  waiting for transfers between devices  198 us (49%)
  Pallas kernels  159 us (40%)
  starting transfers between devices  16.3 us (4%)
  between operations  13.5 us (3%)
  local copies, waits for them, and re-layouts  11.9 us (3%)
    psum x1, waiting for transfers between devices, on_device(): sums = lax.psum(sums, 'rows')  154 us
    pallas_call x1, Pallas kernels, update_and_send(): pl.pallas_call(functools.partial(update_kernel, n, chunk), out_shape=jax....  101 us
    pallas_call x1, Pallas kernels, solve(): pl.pallas_call(solve_kernel, out_shape=jax.ShapeDtypeStruct((ne, ne), jnp...  57.6 us
    all_to_all x1, waiting for transfers between devices, on_device(): lax.all_to_all(predicted, 'rows', split_axis=1, concat_axis=0, tiled=True)  23.8 us
    all_to_all x1, waiting for transfers between devices, on_device(): lax.all_to_all(noise, 'rows', split_axis=1, concat_axis=0, tiled=True)  20.2 us
  transfers between devices with their start and end apart: 4, of which 3 were waited for; matrix products, arithmetic and copies ran while one was open for 3% of the time, Pallas kernels for 14%

profile of v1, /device:TPU:13, one launch (start us, length us, event | category | flops | bytes accessed | tf_op | source)
XLA Modules:
  0.0 401.7 jit_solution(15477536212707820793)
XLA Ops:
  6.5 0.0 copy-start
  6.5 2.4 copy.22
  8.9 6.5 %all-to-all-start = ((bf16[32,16,1024]{2,0,1:T(8,128)(2,1)}), bf16[32,16,1024]{2,0,1:T(8,128)(2,1)S(1)}, u32[]{:S(2)}, u32[]{:S(2)}) async-start(bf16[32,16,1024]{2,0,1:T(8,128)(2,1)} %bitcast.34), calls=%async_computation | async-start | bytes 2097152 | tf_op jit(solution)/shard_map/all_to_all | solution.py:179
  15.4 0.0 copy-done
  15.4 1.1 copy.21
  16.5 23.8 %all-to-all-done = bf16[32,16,1024]{2,0,1:T(8,128)(2,1)S(1)} async-done(((bf16[32,16,1024]{2,0,1:T(8,128)(2,1)}), bf16[32,16,1024]{2,0,1:T(8,128)(2,1)S(1)}, u32[]{:S(2)}, u32[]{:S(2)}) %all-to-all-start) | async-done | bytes 1048608 | tf_op jit(solution)/shard_map/all_to_all | solution.py:179
  40.3 4.8 %all-to-all-start.1 = ((bf16[32,16,1024]{2,0,1:T(8,128)(2,1)}), bf16[32,16,1024]{2,0,1:T(8,128)(2,1)S(1)}, u32[]{:S(2)}, u32[]{:S(2)}) async-start(bf16[32,16,1024]{2,0,1:T(8,128)(2,1)} %bitcast.33), calls=%async_computation.1 | async-start | bytes 2097152 | tf_op jit(solution)/shard_map/all_to_all | solution.py:180
  45.1 4.7 %copy.20 = bf16[4,16,8,4096]{3,2,0,1:T(8,128)(2,1)} copy(bf16[4,16,8,4096]{3,2,1,0:T(8,128)(2,1)} %bitcast.36) | data formatting | bytes 8388608 | tf_op jit(solution)/shard_map/all_to_all | solution.py:182
  49.8 20.2 %all-to-all-done.1 = bf16[32,16,1024]{2,0,1:T(8,128)(2,1)S(1)} async-done(((bf16[32,16,1024]{2,0,1:T(8,128)(2,1)}), bf16[32,16,1024]{2,0,1:T(8,128)(2,1)S(1)}, u32[]{:S(2)}, u32[]{:S(2)}) %all-to-all-start.1) | async-done | bytes 1048608 | tf_op jit(solution)/shard_map/all_to_all | solution.py:180
  70.0 0.0 copy-start.1
  70.0 0.0 copy-start.2
  70.0 5.0 %all-to-all-start.2 = ((bf16[32,16,4096]{2,0,1:T(8,128)(2,1)}), bf16[32,16,4096]{2,0,1:T(8,128)(2,1)}, u32[]{:S(2)}, u32[]{:S(2)}) async-start(bf16[32,16,4096]{2,0,1:T(8,128)(2,1)} %bitcast.35), calls=%async_computation.2 | async-start | bytes 8388608 | tf_op jit(solution)/shard_map/all_to_all | solution.py:182
  74.9 0.0 all-reduce.2.cloned.1.call-start
  75.0 0.0 copy-done.1
  75.0 0.2 convert_reduce_fusion
  75.2 0.0 copy-done.2
  75.2 0.6 fusion.4
  75.8 2.6 fusion
  78.5 0.0 all-reduce.2.cloned.1.call-update
  78.5 153.7 %all-reduce.2.cloned.1.call-done = f32[1024,512]{1,0:T(8,128)} async-done(((f32[1024,512]{1,0:T(8,128)}), f32[1024,512]{1,0:T(8,128)}) %all-reduce.2.cloned.1.call-update) | async-done | bytes 2097168 | tf_op jit(solution)/shard_map/psum | solution.py:193
  232.2 1.7 fusion.9
  233.9 57.6 %solve.1.weights_t_ref = bf16[512,512]{1,0:T(8,128)(2,1)S(1)} custom-call(f32[512,512]{1,0:T(8,128)S(1)} %get-tuple-element.6.gram_ref, f32[512,512]{1,0:T(8,128)S(1)} %get-tuple-element.5.cross_t_ref), custom_call_target="tpu_custom_call" | custom-call | flops 5368709120 | bytes 209715200 | tf_op jit(solution)/shard_map/solve/pallas_call | solution.py:64
  291.5 0.0 all-to-all-done.2
  291.5 101.3 %update.1 = bf16[32,65536]{1,0:T(8,128)(2,1)S(1)} custom-call(bf16[512,512]{1,0:T(8,128)(2,1)S(1)} %solve.1.weights_t_ref, bf16[512,4096]{1,0:T(8,128)(2,1)} %bitcast.6.params_ref), custom_call_target="tpu_custom_call" | custom-call | tf_op jit(solution)/shard_map/update/pallas_call | solution.py:154
  392.8 2.0 copy.25
  (2 shorter events, 0.0 us)
Async XLA Ops:
  6.5 8.9 %copy-start = (bf16[32,16384]{1,0:T(8,128)(2,1)S(1)}, bf16[32,16384]{1,0:T(8,128)(2,1)}, u32[]{:S(2)}) copy-start(bf16[32,16384]{1,0:T(8,128)(2,1)} %param.7) | copy-start | bytes 3145732
  8.9 31.4 %all-to-all-start = ((bf16[32,16,1024]{2,0,1:T(8,128)(2,1)}), bf16[32,16,1024]{2,0,1:T(8,128)(2,1)S(1)}, u32[]{:S(2)}, u32[]{:S(2)}) async-start(bf16[32,16,1024]{2,0,1:T(8,128)(2,1)} %bitcast.34), calls=%async_computation | async-start | bytes 2097152 | tf_op jit(solution)/shard_map/all_to_all | solution.py:179
  40.3 29.7 %all-to-all-start.1 = ((bf16[32,16,1024]{2,0,1:T(8,128)(2,1)}), bf16[32,16,1024]{2,0,1:T(8,128)(2,1)S(1)}, u32[]{:S(2)}, u32[]{:S(2)}) async-start(bf16[32,16,1024]{2,0,1:T(8,128)(2,1)} %bitcast.33), calls=%async_computation.1 | async-start | bytes 2097152 | tf_op jit(solution)/shard_map/all_to_all | solution.py:180
  70.0 5.0 %copy-start.1 = (f32[1024]{0:T(1024)S(1)}, f32[1024]{0:T(1024)}, u32[]{:S(2)}) copy-start(f32[1024]{0:T(1024)} %param.9) | copy-start | bytes 12292
  70.0 5.2 %copy-start.2 = (f32[1024]{0:T(1024)S(1)}, f32[1024]{0:T(1024)}, u32[]{:S(2)}) copy-start(f32[1024]{0:T(1024)} %param.8) | copy-start | bytes 12292
  70.0 221.5 %all-to-all-start.2 = ((bf16[32,16,4096]{2,0,1:T(8,128)(2,1)}), bf16[32,16,4096]{2,0,1:T(8,128)(2,1)}, u32[]{:S(2)}, u32[]{:S(2)}) async-start(bf16[32,16,4096]{2,0,1:T(8,128)(2,1)} %bitcast.35), calls=%async_computation.2 | async-start | bytes 8388608 | tf_op jit(solution)/shard_map/all_to_all | solution.py:182
  74.9 157.3 %all-reduce.2.cloned.1.call-start = ((), (), s32[]{:S(2)}) async-start(), calls=%async_computation.3 | async-start | bytes 4194304 | tf_op jit(solution)/shard_map/psum | solution.py:193
Sparse Core Ops, SparseCore 0:
  79.3 152.8 all-reduce.1

commit v2 on v0

v2 whole, which is shorter than its diff:
```python
import functools
import math

import jax
import jax.numpy as jnp
from jax import lax
from jax.experimental import pallas as pl
from jax.experimental.pallas import tpu as pltpu
from jax.sharding import PartitionSpec as P

damping = 21.0
BLOCK = 128
HIGHEST = lax.Precision.HIGHEST


def sweep_block(m):
    size = m.shape[0]
    rows = lax.broadcasted_iota(jnp.int32, m.shape, 0)
    columns = lax.broadcasted_iota(jnp.int32, m.shape, 1)
    for k in range(size):
        row = m[k : k + 1, :]
        column = m[:, k : k + 1]
        inverse = 1.0 / m[k : k + 1, k : k + 1]
        scaled = row * inverse
        swept = m - column * scaled
        swept = jnp.where(columns == k, column * inverse, swept)
        edge = jnp.where(columns[k : k + 1] == k, -inverse, scaled)
        m = jnp.where(rows == k, edge, swept)
    return m


MESH = pl.DeviceIdType.MESH


def smoother_kernel(
    n,
    chunk,
    early,
    members_ref,
    predicted_ref,
    noise_ref,
    observed_ref,
    spread_ref,
    out_ref,
    response,
    jitter,
    both,
    sums,
    arrived,
    full,
    inverse,
    params_ref,
    held,
    data_send,
    data_recv,
    own_data,
    tree_send,
    tree_recv,
    member_send,
    member_recv,
    own_member,
    out_send,
    out_recv,
    own_out,
):
    me = lax.axis_index("rows")
    local = members_ref.shape[0]
    ne = n * local
    cells = members_ref.shape[1] // n
    data = predicted_ref.shape[1] // n
    count = cells // chunk
    levels = n.bit_length() - 1
    scale = 1.0 / math.sqrt(ne - 1)
    barrier = pltpu.get_barrier_semaphore()

    def each_peer(do):
        def one(s, carry):
            do(s, lax.rem(me + s, n))
            return carry

        lax.fori_loop(1, n, one, 0)

    def span(start, size):
        return pl.ds(pl.multiple_of(start, size), size)

    each_peer(
        lambda s, peer: pl.semaphore_signal(
            barrier, inc=1, device_id={"rows": peer}, device_id_type=MESH
        )
    )
    pl.semaphore_wait(barrier, n - 1)

    def remote(source, target, send, recv, peer):
        return pltpu.make_async_remote_copy(
            src_ref=source,
            dst_ref=target,
            send_sem=send,
            recv_sem=recv,
            device_id={"rows": peer},
            device_id_type=MESH,
        )

    fields = ((predicted_ref, response), (noise_ref, jitter))

    def data_copy(which, s, peer):
        source, target = fields[which]
        return remote(
            source.at[:, span(peer * data, data)],
            target.at[me],
            data_send.at[which, s],
            data_recv.at[which, s],
            peer,
        )

    def own_data_copy(which):
        source, target = fields[which]
        return pltpu.make_async_copy(
            source.at[:, span(me * data, data)], target.at[me], own_data.at[which]
        )

    def member_copy(c, s, peer):
        return remote(
            members_ref.at[:, span(peer * cells + c * chunk, chunk)],
            params_ref.at[me, :, span(c * chunk, chunk)],
            member_send.at[c, s],
            member_recv.at[c, s],
            peer,
        )

    def own_member_copy(c):
        return pltpu.make_async_copy(
            members_ref.at[:, span(me * cells + c * chunk, chunk)],
            params_ref.at[me, :, span(c * chunk, chunk)],
            own_member.at[c],
        )

    def out_copy(c, s, peer):
        return remote(
            held.at[peer, :, span(c * chunk, chunk)],
            out_ref.at[:, span(me * cells + c * chunk, chunk)],
            out_send.at[c, s],
            out_recv.at[c, s],
            peer,
        )

    def own_out_copy(c):
        return pltpu.make_async_copy(
            held.at[me, :, span(c * chunk, chunk)],
            out_ref.at[:, span(me * cells + c * chunk, chunk)],
            own_out.at[c],
        )

    for which in range(2):
        own_data_copy(which).start()
        each_peer(lambda s, peer: data_copy(which, s, peer).start())

    def send_members(c, carry):
        own_member_copy(c).start()
        each_peer(lambda s, peer: member_copy(c, s, peer).start())
        return carry

    own_data_copy(0).wait()
    each_peer(lambda s, peer: data_copy(0, s, peer).wait())
    piece = min(data, 256)

    def whiten(p, carry):
        here = span(p * piece, piece)
        values = response[:, :, here].astype(jnp.float32).reshape(ne, piece)
        mean = jnp.sum(values, axis=0, keepdims=True) * (1.0 / ne)
        both[:ne, here] = ((values - mean) * (scale / spread_ref[:, here])).astype(jnp.bfloat16)
        return carry

    lax.fori_loop(0, data // piece, whiten, 0)
    rows = 256

    def multiply(b, carry):
        here = span(b * rows, rows)
        sums[here, :] = lax.dot_general(
            both[here, :data], both[:ne, :data], (((1,), (1,)), ((), ())), preferred_element_type=jnp.float32
        )
        return carry

    lax.fori_loop(0, ne // rows, multiply, 0)
    own_data_copy(1).wait()
    each_peer(lambda s, peer: data_copy(1, s, peer).wait())
    lax.fori_loop(0, early, send_members, 0)

    def residual(p, carry):
        here = span(p * piece, piece)
        values = response[:, :, here].astype(jnp.float32).reshape(ne, piece)
        noise = jitter[:, :, here].astype(jnp.float32).reshape(ne, piece)
        both[ne:, here] = ((observed_ref[:, here] - values) / spread_ref[:, here] + noise).astype(
            jnp.bfloat16
        )
        return carry

    lax.fori_loop(0, data // piece, residual, 0)
    lax.fori_loop(ne // rows, 2 * ne // rows, multiply, 0)

    orders = [list(range(levels)), [0] + list(range(2, levels)) + [1]][: 2 if levels > 1 else 1]
    width = ne // len(orders)
    plans = []
    for order in orders:
        start, plan = 0, []
        for level, b in enumerate(order):
            half = ne >> level
            bit = lax.rem(me // (1 << b), 2)
            plan.append((half, start + bit * half, start + (1 - bit) * half, me + (1 - 2 * bit) * (1 << b)))
            start = start + bit * half
        plans.append(plan)

    def scatter(level, h):
        half, mine, other, partner = plans[h][level]
        columns = pl.ds(h * width, width)
        return remote(
            sums.at[span(other, half), columns],
            arrived.at[pl.ds(2 * ne - 2 * half, half), columns],
            tree_send.at[0, level, h],
            tree_recv.at[0, level, h],
            partner,
        )

    def gather(level, h):
        half, mine, other, partner = plans[h][level]
        columns = pl.ds(h * width, width)
        here = full.at[span(mine, half), columns]
        return remote(here, here, tree_send.at[1, level, h], tree_recv.at[1, level, h], partner)

    halves = range(len(orders))
    for h in halves:
        scatter(0, h).start()
    for level in range(levels):
        for h in halves:
            half, mine, other, partner = plans[h][level]
            columns = pl.ds(h * width, width)
            scatter(level, h).wait()
            total = sums[span(mine, half), columns] + arrived[pl.ds(2 * ne - 2 * half, half), columns]
            if level < levels - 1:
                sums[span(mine, half), columns] = total
                scatter(level + 1, h).start()
            else:
                full[span(mine, half), columns] = total
                gather(level, h).start()
    for level in reversed(range(levels)):
        for h in halves:
            gather(level, h).wait()
            if level:
                gather(level - 1, h).start()
    lax.fori_loop(early, count, send_members, 0)

    eye = lax.broadcasted_iota(jnp.int32, (ne, ne), 0) == lax.broadcasted_iota(
        jnp.int32, (ne, ne), 1
    )
    inverse[...] = full[:ne, :] + jnp.where(eye, damping, 0.0)

    def exact(a, b):
        return jnp.dot(a, b, precision=HIGHEST, preferred_element_type=jnp.float32)

    def step(block, carry):
        here = span(block * BLOCK, BLOCK)
        negative = sweep_block(inverse[here, here])
        column = inverse[:, here]
        scaled = -exact(negative, inverse[here, :])
        scaled_column = -exact(column, negative)
        inverse[...] = inverse[...] - exact(column, scaled)
        inverse[here, :] = scaled
        inverse[:, here] = scaled_column
        inverse[here, here] = negative
        return carry

    lax.fori_loop(0, ne // BLOCK, step, 0)
    both[:ne, :ne] = (-exact(full[ne:, :], inverse[...])).astype(jnp.bfloat16)

    def update(c, carry):
        own_member_copy(c).wait()
        each_peer(lambda s, peer: member_copy(c, s, peer).wait())
        here = span(c * chunk, chunk)
        params = params_ref[:, :, here].astype(jnp.float32).reshape(ne, chunk)
        mean = jnp.sum(params, axis=0, keepdims=True) * (1.0 / ne)
        anomaly = ((params - mean) * scale).astype(jnp.bfloat16)
        change = jnp.dot(both[:ne, :ne], anomaly, preferred_element_type=jnp.float32)
        held[:, :, here] = (params + change).reshape(n, local, chunk).astype(jnp.bfloat16)
        each_peer(lambda s, peer: out_copy(c, s, peer).start())
        own_out_copy(c).start()
        return carry

    lax.fori_loop(0, count, update, 0)

    def finish(c, carry):
        each_peer(lambda s, peer: out_copy(c, s, peer).wait())
        own_out_copy(c).wait()
        return carry

    lax.fori_loop(0, count, finish, 0)


def on_device(members, predicted, noise, observed, observation_spread):
    n = lax.axis_size("rows")
    local = members.shape[0]
    ne = local * n
    cells = members.shape[1] // n
    data = predicted.shape[1] // n
    levels = n.bit_length() - 1
    count = 4
    chunk = cells // count
    hbm = pl.BlockSpec(memory_space=pl.ANY)
    vmem = pl.BlockSpec(memory_space=pltpu.VMEM)
    dma = pltpu.SemaphoreType.DMA
    return pl.pallas_call(
        functools.partial(smoother_kernel, n, chunk, 1),
        out_shape=jax.ShapeDtypeStruct((local, n * cells), jnp.bfloat16),
        in_specs=[hbm, hbm, hbm, vmem, vmem],
        out_specs=hbm,
        scratch_shapes=[
            pltpu.VMEM((n, local, data), jnp.bfloat16),
            pltpu.VMEM((n, local, data), jnp.bfloat16),
            pltpu.VMEM((2 * ne, max(data, ne)), jnp.bfloat16),
            pltpu.VMEM((2 * ne, ne), jnp.float32),
            pltpu.VMEM((2 * ne, ne), jnp.float32),
            pltpu.VMEM((2 * ne, ne), jnp.float32),
            pltpu.VMEM((ne, ne), jnp.float32),
            pltpu.VMEM((n, local, cells), jnp.bfloat16),
            pltpu.VMEM((n, local, cells), jnp.bfloat16),
            dma((2, n)),
            dma((2, n)),
            dma((2,)),
            dma((2, levels, 2)),
            dma((2, levels, 2)),
            dma((count, n)),
            dma((count, n)),
            dma((count,)),
            dma((count, n)),
            dma((count, n)),
            dma((count,)),
        ],
        compiler_params=pltpu.CompilerParams(
            collective_id=0, has_side_effects=True, vmem_limit_bytes=50 * 2**20
        ),
        name="smoother",
    )(members, predicted, noise, observed[None], observation_spread[None])


def solution(mesh):
    in_specs = (
        P("rows", "fields"),
        P("rows", "fields"),
        P("rows", "fields"),
        P(("fields", "rows")),
        P(("fields", "rows")),
    )
    return jax.shard_map(
        on_device, mesh=mesh, in_specs=in_specs, out_specs=P("rows", "fields"), check_vma=False
    )
```

time: 540 us -> 284 us (0.53); the launches traced: 534 us -> 284 us
  Pallas kernels: 0 us -> 275 us
  waiting for transfers between devices: 192 us -> 0 us
  other arithmetic: 134 us -> 0 us
  blocking collectives: 100 us -> 0 us
  local copies, waits for them, and re-layouts: 52.2 us -> 8.29 us
  matrix products: 22.4 us -> 0 us
  starting transfers between devices: 16.8 us -> 0 us
  between operations: 16.6 us -> 0.01 us
    pallas_call x0 -> x1, Pallas kernels: none -> 275 us  [on_device(): pl.pallas_call(functools.partial(smoother_kernel, n, chunk, 1), out_shape...]
    psum x1 -> x0, waiting for transfers between devices: 143 us -> none  [on_device(): gram_total, cross_total = lax.psum((gram_matrix, cross_terms), 'rows')]
    another operation x18 -> x0, other arithmetic: 119 us -> none  [the longest x14 78.8 us: on_device(): factor = jnp.linalg.cholesky(gram_total + damping * identity)]
    all_to_all x1 -> x0, blocking collectives: 100 us -> none  [on_device(): lax.all_to_all(renewed, 'rows', split_axis=0, concat_axis=1, tiled=True)]
    all_to_all x3 -> x0, waiting for transfers between devices: 48.4 us -> none  [the longest x1 24.6 us: on_device(): lax.all_to_all(noise, 'rows', split_axis=1, concat_axis=0, tiled=True)]
    unnamed x12 -> x9, local copies, waits for them, and re-layouts: 34.1 us -> 8.29 us
    all_to_all x3 -> x0, starting transfers between devices: 16.8 us -> none  [the longest x1 6.65 us: on_device(): lax.all_to_all(predicted, 'rows', split_axis=1, concat_axis=0, tiled=True)]
    another operation x20 -> x0, matrix products: 12.2 us -> none  [the longest x14 9.91 us: on_device(): jax.scipy.linalg.cho_solve((factor, True), cross_total).astype(jnp.bfloat16)]
  transfers between devices with their start and end apart: 4 -> 0, of which waited for: 3 -> 0; matrix products, arithmetic and copies ran while one was open for 28% -> 0% of each run, Pallas kernels for 0% -> 0%
where the time goes in v2:
time: 284 us
  Pallas kernels  275 us (97%)
  local copies, waits for them, and re-layouts  8.29 us (3%)
    pallas_call x1, Pallas kernels, on_device(): pl.pallas_call(functools.partial(smoother_kernel, n, chunk, 1), out_shape...  275 us
    unnamed x9, local copies, waits for them, and re-layouts  8.29 us

profile of v2, /device:TPU:13, one launch (start us, length us, event | category | flops | bytes accessed | tf_op | source)
XLA Modules:
  0.0 283.5 jit_solution(11837920474078587015)
XLA Ops:
  0.0 0.0 copy-start
  0.0 1.2 copy-done
  1.2 0.0 copy-start.1
  1.2 1.2 copy-done.1
  2.5 0.0 copy-start.2
  2.5 0.7 copy-done.2
  3.1 0.0 copy-start.3
  3.1 0.7 copy-done.3
  3.8 275.2 %smoother.1 = bf16[32,65536]{1,0:T(8,128)(2,1)} custom-call(bf16[32,65536]{1,0:T(8,128)(2,1)} %members_ref.1, bf16[32,16384]{1,0:T(8,128)(2,1)S(1)} %copy-done, bf16[32,16384]{1,0:T(8,128)(2,1)S(1)} %copy-done.1, f32[1,1024]{1,0:T(1,128)S(1)} %bitcast.2, f32[1,1024]{1,0:T(1,128)S(1)} %bitcast.3), custom_call_target="tpu_custom_call" | custom-call | tf_op jit(solution)/shard_map/smoother/pallas_call | solution.py:309
  279.0 4.5 %copy.7 = bf16[32,65536]{1,0:T(8,128)(2,1)} copy(bf16[32,65536]{1,0:T(8,128)(2,1)} %smoother.1) | data formatting | bytes 8388608
Async XLA Ops:
  0.0 1.2 copy-start
  1.2 1.2 copy-start.1
  2.5 0.7 copy-start.2
  3.1 0.7 copy-start.3

commit v3 on v2

--- a/solution.py
+++ b/solution.py
@@ -17,15 +17,18 @@
     size = m.shape[0]
     rows = lax.broadcasted_iota(jnp.int32, m.shape, 0)
     columns = lax.broadcasted_iota(jnp.int32, m.shape, 1)
-    for k in range(size):
-        row = m[k : k + 1, :]
-        column = m[:, k : k + 1]
-        inverse = 1.0 / m[k : k + 1, k : k + 1]
-        scaled = row * inverse
-        swept = m - column * scaled
-        swept = jnp.where(columns == k, column * inverse, swept)
-        edge = jnp.where(columns[k : k + 1] == k, -inverse, scaled)
-        m = jnp.where(rows == k, edge, swept)
+    lane = columns[:1]
+    for k in range(0, size, 2):
+        row0, row1 = m[k : k + 1, :], m[k + 1 : k + 2, :]
+        column0, column1 = m[:, k : k + 1], m[:, k + 1 : k + 2]
+        a, b, c = m[k : k + 1, k : k + 1], m[k : k + 1, k + 1 : k + 2], m[k + 1 : k + 2, k + 1 : k + 2]
+        reciprocal = 1.0 / (a * c - b * b)
+        i00, i01, i11 = c * reciprocal, -b * reciprocal, a * reciprocal
+        scaled0 = jnp.where(lane == k, -i00, jnp.where(lane == k + 1, -i01, i00 * row0 + i01 * row1))
+        scaled1 = jnp.where(lane == k, -i01, jnp.where(lane == k + 1, -i11, i01 * row0 + i11 * row1))
+        kept = jnp.where((columns == k) | (columns == k + 1), 0.0, m)
+        swept = kept - column0 * scaled0 - column1 * scaled1
+        m = jnp.where(rows == k, scaled0, jnp.where(rows == k + 1, scaled1, swept))
     return m
 
 
@@ -150,14 +153,39 @@
             own_out.at[c],
         )
 
+    for c in range(count):
+        own_member_copy(c).start()
     for which in range(2):
         own_data_copy(which).start()
         each_peer(lambda s, peer: data_copy(which, s, peer).start())
 
-    def send_members(c, carry):
-        own_member_copy(c).start()
-        each_peer(lambda s, peer: member_copy(c, s, peer).start())
-        return carry
+    slugs = 4 * count
+    part = chunk // 4
+
+    def send_members(slug, carry):
+        c = slug // 4
+        offset = c * chunk + lax.rem(slug, 4) * part
+
+        def one(s, peer):
+            remote(
+                members_ref.at[:, span(peer * cells + offset, part)],
+                params_ref.at[me, :, span(offset, part)],
+                member_send.at[c, s],
+                member_recv.at[c, s],
+                peer,
+            ).start()
+
+        each_peer(one)
+        return carry
+
+    sent = 0
+
+    def slip_members(more):
+        nonlocal sent
+        more = min(more, slugs - sent)
+        if more:
+            lax.fori_loop(sent, sent + more, send_members, 0)
+        sent += more
 
     own_data_copy(0).wait()
     each_peer(lambda s, peer: data_copy(0, s, peer).wait())
@@ -183,7 +211,7 @@
     lax.fori_loop(0, ne // rows, multiply, 0)
     own_data_copy(1).wait()
     each_peer(lambda s, peer: data_copy(1, s, peer).wait())
-    lax.fori_loop(0, early, send_members, 0)
+    slip_members(early)
 
     def residual(p, carry):
         here = span(p * piece, piece)
@@ -241,12 +269,15 @@
             else:
                 full[span(mine, half), columns] = total
                 gather(level, h).start()
+        slip_members(1)
     for level in reversed(range(levels)):
         for h in halves:
             gather(level, h).wait()
             if level:
                 gather(level - 1, h).start()
-    lax.fori_loop(early, count, send_members, 0)
+        if level:
+            slip_members(1)
+    slip_members(slugs)
 
     eye = lax.broadcasted_iota(jnp.int32, (ne, ne), 0) == lax.broadcasted_iota(
         jnp.int32, (ne, ne), 1

time: 284 us -> 293 us (1.032)
  Pallas kernels: 275 us -> 284 us
    pallas_call x1, Pallas kernels: 275 us -> 284 us  [on_device(): pl.pallas_call(functools.partial(smoother_kernel, n, chunk, 1), out_shape...]
where the time goes in v3:
time: 293 us; the launch traced here: 292 us
  Pallas kernels  284 us (97%)
  local copies, waits for them, and re-layouts  8.29 us (3%)
    pallas_call x1, Pallas kernels, on_device(): pl.pallas_call(functools.partial(smoother_kernel, n, chunk, 1), out_shape...  284 us
    unnamed x9, local copies, waits for them, and re-layouts  8.29 us

profile of v3, /device:TPU:13, one launch (start us, length us, event | category | flops | bytes accessed | tf_op | source)
XLA Modules:
  0.0 292.2 jit_solution(8499176912299370510)
XLA Ops:
  0.0 0.0 copy-start
  0.0 1.2 copy-done
  1.2 0.0 copy-start.1
  1.2 1.2 copy-done.1
  2.5 0.0 copy-start.2
  2.5 0.7 copy-done.2
  3.1 0.0 copy-start.3
  3.1 0.7 copy-done.3
  3.8 283.9 %smoother.1 = bf16[32,65536]{1,0:T(8,128)(2,1)} custom-call(bf16[32,65536]{1,0:T(8,128)(2,1)} %members_ref.1, bf16[32,16384]{1,0:T(8,128)(2,1)S(1)} %copy-done, bf16[32,16384]{1,0:T(8,128)(2,1)S(1)} %copy-done.1, f32[1,1024]{1,0:T(1,128)S(1)} %bitcast.2, f32[1,1024]{1,0:T(1,128)S(1)} %bitcast.3), custom_call_target="tpu_custom_call" | custom-call | tf_op jit(solution)/shard_map/smoother/pallas_call | solution.py:340
  287.7 4.5 %copy.7 = bf16[32,65536]{1,0:T(8,128)(2,1)} copy(bf16[32,65536]{1,0:T(8,128)(2,1)} %smoother.1) | data formatting | bytes 8388608
Async XLA Ops:
  0.0 1.2 copy-start
  1.2 1.2 copy-start.1
  2.5 0.7 copy-start.2
  3.1 0.7 copy-start.3
